TPU v7x, 128 devices: a 2x2x16 block of a 8x8x16 slice. The times are simulated.
128 devices in a mesh: groups: 4 (over y, x), seq: 16 (over z), head: 2 (over core).
Axes of the slice: x: 2, y: 2, z: 16, core: 2. Of those that a mesh axis runs over, the one named last changes fastest.
The devices are a block of a 8x8x16 slice.
Arguments:
- queries: bfloat16 [16384, 3584], P(('groups', 'seq'), 'head'), parts along dimension 0, may hold values from -30 to 30
- current_keys: bfloat16 [16384, 512], P(('groups', 'seq'), 'head'), parts along dimension 0, may hold values from -6 to 6
- current_values: bfloat16 [16384, 512], P(('groups', 'seq'), 'head'), parts along dimension 0, may hold values from -6 to 6
- stored_keys: bfloat16 [16384, 2, 512], P(('groups', 'seq'), None, 'head'), parts along dimension 0, may hold values from -22 to 22
- stored_values: bfloat16 [16384, 2, 512], P(('groups', 'seq'), None, 'head'), parts along dimension 0, may hold values from -6 to 6
- remap_table: int32 [3, 256], P(None, ('groups', 'seq')), parts along dimension 1, may hold values from 0 to 4095
- block_table: int32 [1024], P('groups'), parts along dimension 0, may hold values from 0 to 15, as said below
Outputs:
- attended: bfloat16 [16384, 3584], P(('groups', 'seq'), 'head'), parts along dimension 0
- paged_keys: bfloat16 [4, 1024, 2048], P('head', ('groups', 'seq')), parts along dimension 1
- paged_values: bfloat16 [4, 1024, 2048], P('head', ('groups', 'seq')), parts along dimension 1
There are 4 independent parts, one for each index of `groups`. A program takes and returns all parts, laid end to end along the dimension named above; each array names one. Nothing has to cross between parts.
Inputs may be any that keep to these rules, and one draw needn't show every extreme that they name: `block_table`: the entries of the blocks b that share b modulo 16 are a permutation of 0 to 15.
All inputs are finite; a program needn't handle non-finite values.
Results may differ from a plain program's by a relative error of at most 0.012.
The roundings to bfloat16 on the way count: a program that leaves them out, or rounds other values in their place, can miss the bound.
Values may be sent and summed in bfloat16 or wider, within the bound.
A program may use at most 128 MiB of HBM per device.

v0:
```python
import math

import jax
import jax.numpy as jnp
from jax import lax
from jax.sharding import PartitionSpec as P

HEAD_SIZE = 128
PRIOR_SEGMENTS = 2
PAGE_TOKENS = 16
QBLK = 64


rope_base = 1000000.0
masked_value = -1e30


def in_one_piece(arrays, axis, dim, along):
    columns = [a.reshape(*a.shape[:along], -1) for a in arrays]
    both = jnp.concatenate(columns, axis=along)
    result, at, gathered = (lax.all_gather(both, axis, axis=dim, tiled=True), 0, [])
    for a, column in zip(arrays, columns):
        slab = result[..., at : at + column.shape[along]]
        gathered.append(slab.reshape(*slab.shape[:along], *a.shape[along:]))
        at += column.shape[along]
    return tuple(gathered)


def apply_rotary(values, token_positions):
    half_dim = values.shape[-1] // 2
    frequency = rope_base ** (-2.0 * jnp.arange(half_dim, dtype=jnp.float32) / values.shape[-1])
    angles = token_positions.astype(jnp.float32)[:, None] * frequency[None, :]
    cos_table = jnp.cos(angles)[:, None, :]
    sin_table = jnp.sin(angles)[:, None, :]
    first_half = values[..., :half_dim]
    second_half = values[..., half_dim:]
    return jnp.concatenate(
        [
            first_half * cos_table - second_half * sin_table,
            second_half * cos_table + first_half * sin_table,
        ],
        -1,
    )


def update_block(state, query_rows, key_tile, value_tile, allowed):
    running_max, denom, accumulated = state
    scores = jnp.einsum(
        "grd,gkd->grk", query_rows, key_tile, preferred_element_type=jnp.float32
    ) * query_rows.shape[-1] ** (-0.5)
    if allowed is not None:
        scores = jnp.where(allowed[None], scores, masked_value)
    new_max = jnp.maximum(running_max, jnp.max(scores, -1))
    factor = jnp.exp(running_max - new_max)
    weights = jnp.exp(scores - new_max[..., None])
    if allowed is not None:
        weights = jnp.where(allowed[None], weights, 0.0)
    denom = denom * factor + jnp.sum(weights, -1)
    product = jnp.einsum(
        "grk,gkd->grd", weights.astype(jnp.bfloat16), value_tile, preferred_element_type=jnp.float32
    )
    accumulated = accumulated * factor[..., None] + product
    return (new_max, denom, accumulated)


def attend(state, query_rows, keys, values, row_token, last_token, causal):
    kv_local = query_rows.shape[0]
    head_dim = query_rows.shape[-1]
    key_count = keys.shape[0]
    key_block = math.gcd(key_count, 256)

    def step_body(step_index, held_state):
        offset = step_index * key_block
        key_tile = (
            lax.dynamic_slice_in_dim(keys, offset, key_block, 0)
            .reshape(key_block, kv_local, head_dim)
            .transpose(1, 0, 2)
        )
        value_tile = (
            lax.dynamic_slice_in_dim(values, offset, key_block, 0)
            .reshape(key_block, kv_local, head_dim)
            .transpose(1, 0, 2)
        )
        if causal:
            key_index = offset + jnp.arange(key_block, dtype=jnp.int32)
            allowed = key_index[None, :] <= row_token[:, None]
            return lax.cond(
                offset <= last_token,
                lambda inner: update_block(inner, query_rows, key_tile, value_tile, allowed),
                lambda inner: inner,
                held_state,
            )
        return update_block(held_state, query_rows, key_tile, value_tile, None)

    return lax.fori_loop(0, key_count // key_block, step_body, state)


def shards(
    queries, current_keys, current_values, stored_keys, stored_values, remap_table, block_table
):
    tok_rows = queries.shape[0]
    kv_local = current_keys.shape[1] // HEAD_SIZE
    per_group = queries.shape[1] // (kv_local * HEAD_SIZE)
    my_index = lax.axis_index("seq")
    owners = lax.axis_size("seq")
    token_positions = (
        jnp.repeat(remap_table, QBLK, axis=1)
        + (jnp.arange(tok_rows, dtype=jnp.int32) % QBLK)[None, :]
    )
    query_single_float = queries.astype(jnp.float32).reshape(
        tok_rows, kv_local * per_group, HEAD_SIZE
    )
    rotary_output = []
    for segment_kind_index in range(3):
        turned = apply_rotary(query_single_float, token_positions[segment_kind_index]).astype(
            jnp.bfloat16
        )
        rotary_output.append(
            turned.reshape(tok_rows, kv_local, per_group, HEAD_SIZE)
            .transpose(1, 0, 2, 3)
            .reshape(kv_local, tok_rows * per_group, HEAD_SIZE)
        )
    row_count = tok_rows * per_group
    row_token = my_index * tok_rows + jnp.arange(row_count, dtype=jnp.int32) // per_group
    last_token = my_index * tok_rows + tok_rows - 1
    state = (
        jnp.full((kv_local, row_count), masked_value, jnp.float32),
        jnp.zeros((kv_local, row_count), jnp.float32),
        jnp.zeros((kv_local, row_count, HEAD_SIZE), jnp.float32),
    )
    pages_here = tok_rows // PAGE_TOKENS
    paged = jnp.zeros((2, kv_local, pages_here, PAGE_TOKENS * HEAD_SIZE), jnp.bfloat16)
    pieces = in_one_piece((stored_keys, stored_values, current_keys, current_values), "seq", 0, 1)
    held_state = state
    piece_keys = pieces[0]
    piece_values = pieces[1]
    for segment_number in range(PRIOR_SEGMENTS):
        query_rows = rotary_output[2] if segment_number < PRIOR_SEGMENTS - 1 else rotary_output[1]
        held_state = attend(
            held_state,
            query_rows,
            piece_keys[:, segment_number, :],
            piece_values[:, segment_number, :],
            row_token,
            last_token,
            False,
        )
    held_state = attend(
        held_state, rotary_output[0], pieces[2], pieces[3], row_token, last_token, True
    )
    state, paged = (held_state, paged)
    rounds = pages_here // owners
    previous = jnp.stack(
        [stored_keys[:, PRIOR_SEGMENTS - 1, :], stored_values[:, PRIOR_SEGMENTS - 1, :]]
    )
    arranged = (
        previous.reshape(2, rounds, owners, PAGE_TOKENS, kv_local, HEAD_SIZE)
        .transpose(0, 4, 1, 2, 3, 5)
        .reshape(2, kv_local, rounds, owners, PAGE_TOKENS * HEAD_SIZE)
    )
    received = lax.all_to_all(arranged, "seq", split_axis=3, concat_axis=3, tiled=True)
    source_index = jnp.arange(owners, dtype=jnp.int32)[None, :]
    round_index = jnp.arange(rounds, dtype=jnp.int32)[:, None]
    block_index = source_index * pages_here + round_index * owners + my_index
    target = block_table[block_index.reshape(-1)]
    paged = paged.at[:, :, target].set(
        received.reshape(2, kv_local, rounds * owners, PAGE_TOKENS * HEAD_SIZE)
    )
    finished = state[2] / state[1][..., None]
    attended = (
        finished.reshape(kv_local, tok_rows, per_group, HEAD_SIZE)
        .transpose(1, 0, 2, 3)
        .reshape(tok_rows, kv_local * per_group * HEAD_SIZE)
        .astype(jnp.bfloat16)
    )
    return (attended, paged[0], paged[1])


def solution(mesh):
    in_specs = (
        P(("groups", "seq"), "head"),
        P(("groups", "seq"), "head"),
        P(("groups", "seq"), "head"),
        P(("groups", "seq"), None, "head"),
        P(("groups", "seq"), None, "head"),
        P(None, ("groups", "seq")),
        P("groups"),
    )
    out_specs = (
        P(("groups", "seq"), "head"),
        P("head", ("groups", "seq"), None),
        P("head", ("groups", "seq"), None),
    )
    return jax.shard_map(shards, mesh=mesh, in_specs=in_specs, out_specs=out_specs, check_vma=False)
```

profile of v0, /device:TPU:1988, one launch (start us, length us, event | category | flops | bytes accessed | tf_op | source)
XLA Modules:
  0.0 455.2 jit_solution(5095701408847639468)
XLA Ops:
  15.5 7.5 %all-to-all-start = ((bf16[2,2,1,16,2048]{4,1,0,2,3:T(2,128)(2,1)}), bf16[2,2,1,16,2048]{4,1,0,2,3:T(2,128)(2,1)S(1)}, u32[]{:S(2)}, u32[]{:S(2)}) async-start(bf16[2,2,1,16,2048]{4,1,0,2,3:T(2,128)(2,1)} %reshape.362), calls=%async_computation | async-start | bytes 524288 | tf_op jit(solution)/shard_map/all_to_all | solution.py:161
  24.6 2.2 subtract_convert_fusion
  28.1 2.2 copy.87
  30.3 2.3 copy.88
  32.7 2.2 copy.85
  37.4 3.7 copy.83
  41.1 2.2 copy.84
  48.3 139.1 %all-gather.2.cloned.1.call-done = bf16[4096,1536]{0,1:T(8,128)(2,1)} async-done(((bf16[256,1536]{0,1:T(8,128)(2,1)}), bf16[4096,1536]{0,1:T(8,128)(2,1)}) %all-gather.2.cloned.1.call-update) | async-done | bytes 12582928 | tf_op jit(solution)/shard_map/all_gather | solution.py:21
  187.4 4.0 fusion.37
  191.4 3.4 slice_bitcast_fusion
  194.8 88.5 %while.55 = (s32[]{:T(128)}, f32[2,1792]{1,0:T(2,128)S(1)}, f32[2,1792]{1,0:T(2,128)S(1)}, f32[2,1792,128]{2,1,0:T(8,128)S(1)}, bf16[4096,256]{0,1:T(8,128)(2,1)...) while((s32[]{:T(128)}, f32[2,1792]{1,0:T(2,128)S(1)}, ...), condition=%wide.region_3.4_spmd.clone, body=%wide.region_0.3_spmd.clone.sunk | while | flops 478496256 | bytes 17137844 | solution.py:95
  234.8 1.8 bitcast_reduce_fusion.5
  283.4 69.5 %while.53 = (s32[]{:T(128)}, f32[2,1792]{1,0:T(2,128)S(1)}, f32[2,1792]{1,0:T(2,128)S(1)}, f32[2,1792,128]{2,1,0:T(8,128)S(1)}, bf16[4096,256]{0,1:T(8,128)(2,1)...) while((s32[]{:T(128)}, f32[2,1792]{1,0:T(2,128)S(1)}, ...), condition=%wide.region_7.8_spmd, body=%wide.region_4.7_spmd.sunk | while | flops 478026752 | bytes 17137824 | solution.py:95
  352.9 4.7 %fusion.36 = (bf16[4096,256]{0,1:T(8,128)(2,1)}, bf16[4096,256]{0,1:T(8,128)(2,1)}) fusion(bf16[4096,1536]{0,1:T(8,128)(2,1)} %all-gather.2.cloned.1.call-done), kind=kLoop, calls=%fused_computation.98 | loop fusion | bytes 8388608 | tf_op jit(solution)/shard_map/slice | solution.py:23
  357.6 79.7 %while.54 = (s32[]{:T(128)}, f32[2,1792]{1,0:T(2,128)S(1)}, f32[2,1792]{1,0:T(2,128)S(1)}, f32[2,1792,128]{2,1,0:T(8,128)S(1)}, s32[]{:T(128)}, /*index=5*/bf16[...) while((s32[]{:T(128)}, f32[2,1792]{1,0:T(2,128)S(1)}, ...), condition=%wide.region_13.14_spmd.clone, body=%wide.region_8.13_spmd.clone.sunk | while | flops 479419392 | bytes 18524560 | solution.py:95
  358.7 3.9 conditional.3
  363.6 3.9 conditional.3
  368.6 3.9 conditional.3
  373.6 3.9 conditional.3
  378.6 3.9 conditional.3
  383.6 3.9 conditional.3
  388.6 3.9 conditional.3
  393.6 3.9 conditional.3
  398.6 3.9 conditional.3
  403.5 3.9 conditional.3
  408.5 3.9 conditional.3
  413.5 3.9 conditional.3
  418.5 3.9 conditional.3
  423.5 3.9 conditional.3
  428.5 3.9 conditional.3
  433.5 3.9 conditional.3
  437.9 7.6 %copy.89 = bf16[2,1792,128]{2,0,1:T(2,128)(2,1)S(1)} copy(bf16[2,1792,128]{2,1,0:T(8,128)(2,1)S(1)} %divide_convert_fusion) | data formatting | bytes 1835008 | tf_op jit(solution)/shard_map/convert_element_type | solution.py:174
  (576 shorter events, 253.7 us)
Async XLA Ops:
  7.2 36.2 %copy-start = (s32[256]{0:T(256)S(1)}, s32[256]{0:T(256)}, u32[]{:S(2)}) copy-start(s32[256]{0:T(256)} %param.21) | copy-start | bytes 3076
  7.2 5.4 %copy-start.7 = (bf16[256,2,256]{2,1,0:T(2,128)(2,1)S(1)}, bf16[256,2,256]{2,1,0:T(2,128)(2,1)}, u32[]{:S(2)}) copy-start(bf16[256,2,256]{2,1,0:T(2,128)(2,1)} %param.18) | copy-start | bytes 786436
  7.2 180.2 %all-gather.2.cloned.1.call-start = ((), (), s32[]{:S(2)}) async-start(), calls=%async_computation.1 | async-start | bytes 13369344 | tf_op jit(solution)/shard_map/all_gather | solution.py:21
  9.3 4.1 copy-start.8
  12.5 10.4 %copy-start.10 = (s32[3,4]{1,0:T(4,128)S(1)}, s32[3,4]{1,0:T(4,128)}, u32[]{:S(2)}) copy-start(s32[3,4]{1,0:T(4,128)} %param.20) | copy-start | bytes 148
  12.6 10.6 %copy-start.9 = (bf16[256,1792]{1,0:T(8,128)(2,1)S(1)}, bf16[256,1792]{1,0:T(8,128)(2,1)}, u32[]{:S(2)}) copy-start(bf16[256,1792]{1,0:T(8,128)(2,1)} %param.15) | copy-start | bytes 2752516
  15.5 29.8 %all-to-all-start = ((bf16[2,2,1,16,2048]{4,1,0,2,3:T(2,128)(2,1)}), bf16[2,2,1,16,2048]{4,1,0,2,3:T(2,128)(2,1)S(1)}, u32[]{:S(2)}, u32[]{:S(2)}) async-start(bf16[2,2,1,16,2048]{4,1,0,2,3:T(2,128)(2,1)} %reshape.362), calls=%async_computation | async-start | bytes 524288 | tf_op jit(solution)/shard_map/all_to_all | solution.py:161
  30.3 2.3 copy-start.5
  30.3 2.3 copy-start.6
  35.0 1.4 copy-start.3
  35.0 1.4 copy-start.4
  352.9 4.7 %copy-start.2 = (bf16[2,1792,128]{2,1,0:T(8,128)(2,1)S(1)}, bf16[2,1792,128]{2,1,0:T(8,128)(2,1)}, u32[]{:S(2)}) copy-start(bf16[2,1792,128]{2,1,0:T(8,128)(2,1)} %copy.88) | copy-start | bytes 2752516
  437.9 10.5 %copy-start.1 = (s32[256]{0:T(256)S(1)}, s32[256]{0:T(256)}, u32[]{:S(2)}) copy-start(s32[256]{0:T(256)} %param.21) | copy-start | bytes 3076
Sparse Core Ops, SparseCore 0:
  12.7 174.6 all-gather.1
where the time goes:
time: 457 us; the launch traced here: 455 us
  waiting for transfers between devices  140 us (31%)
  matrix products  136 us (30%)
  local copies, waits for them, and re-layouts  104 us (23%)
  other arithmetic  49.2 us (11%)
  between operations  14.3 us (3%)
  starting transfers between devices  7.51 us (2%)
    all_gather x1, waiting for transfers between devices, in_one_piece(): lax.all_gather(both, axis, axis=dim, tiled=True)  139 us
    dot_general x48, matrix products, update_block(): jnp.einsum('grk,gkd->grd', weights.astype(jnp.bfloat16), value_tile, pref...  80.7 us
    dot_general x48, matrix products, update_block(): jnp.einsum('grd,gkd->grk', query_rows, key_tile, preferred_element_type=j...  55.3 us
    dynamic_slice x48, local copies, waits for them, and re-layouts, step_body(): lax.dynamic_slice_in_dim(values, offset, key_block, 0)  47.7 us
    reduce_sum x48, other arithmetic, update_block(): denom = denom * factor + jnp.sum(weights, -1)  32.1 us
    unnamed x32, local copies, waits for them, and re-layouts  12.2 us
  transfers between devices with their start and end apart: 2, of which 2 were waited for; matrix products, arithmetic and copies ran while one was open for 6% of the time, Pallas kernels for 0%

commit v1 on v0

v1 whole, which is shorter than its diff:
```python
import functools

import jax
import jax.numpy as jnp
import numpy as np
from jax import lax
from jax.experimental import pallas as pl
from jax.experimental.pallas import tpu as pltpu
from jax.sharding import PartitionSpec as P

HEAD = 128
PAGE = 16
QBLK = 64
ROPE_BASE = 1000000.0
MASKED = -1e30
MESH = pl.DeviceIdType.MESH
F32 = jnp.float32
BF16 = jnp.bfloat16
SCALE2 = float(HEAD**-0.5 * np.log2(np.e))


def kernel(
    n, groups, per,
    table_ref, remap_ref, freq_ref, q_ref, sk_ref, sv_ref, ck_ref, cv_ref,
    out_ref, pk_ref, pv_ref,
    kv, qrot, acc, m_ref, l_ref,
    local_sem, send_sem, recv_sem,
):
    me = lax.axis_index("seq")
    half = n // 2
    rows = q_ref.shape[0]
    width = groups * HEAD
    right, left = lax.rem(me + 1, n), lax.rem(me + n - 1, n)

    barrier = pltpu.get_barrier_semaphore()
    for neighbour in (left, right):
        pl.semaphore_signal(barrier, inc=1, device_id={"seq": neighbour}, device_id_type=MESH)

    def own(seg, side, g):
        stored, current = ((sk_ref, ck_ref), (sv_ref, cv_ref))[side]
        src = stored if seg < 2 else current
        col = (seg * width if seg < 2 else 0) + g * HEAD
        return pltpu.make_async_copy(
            src.at[:, pl.ds(col, HEAD)], kv.at[me, seg, side, g], local_sem.at[seg, side, g]
        )

    for seg in range(3):
        for side in range(2):
            for g in range(groups):
                own(seg, side, g).start()
    pl.semaphore_wait(barrier, 2)

    def ring(way, slot, seg, side):
        unit = kv.at[slot, seg, side]
        return pltpu.make_async_remote_copy(
            src_ref=unit,
            dst_ref=unit,
            send_sem=send_sem.at[way, slot, seg, side],
            recv_sem=recv_sem.at[slot, seg, side],
            device_id={"seq": (right, left)[way]},
            device_id_type=MESH,
        )

    for seg in range(3):
        for side in range(2):
            for g in range(groups):
                own(seg, side, g).wait()
            ring(0, me, seg, side).start()
            ring(1, me, seg, side).start()

    lanes = lax.broadcasted_iota(jnp.int32, (QBLK, HEAD), 1)
    rising = lax.broadcasted_iota(jnp.int32, (QBLK, HEAD), 0)
    freq = freq_ref[...]

    def rotate(step, _):
        kind = step // (rows // QBLK)
        blk = lax.rem(step, rows // QBLK)
        angle = (rising + remap_ref[kind, blk]).astype(F32) * freq
        cos = jnp.cos(angle)
        sin = jnp.sin(angle)
        sin = jnp.where(lanes < HEAD // 2, -sin, sin)
        at = pl.ds(pl.multiple_of(blk * QBLK, QBLK), QBLK)
        for h in range(groups * per):
            x = q_ref[at, h * HEAD : (h + 1) * HEAD].astype(F32)
            turned = x * cos + pltpu.roll(x, HEAD // 2, 1) * sin
            qrot[2 - kind, h, at, :] = turned.astype(BF16)
        return 0

    lax.fori_loop(0, 3 * (rows // QBLK), rotate, 0)

    m_ref[...] = jnp.full_like(m_ref, MASKED)
    l_ref[...] = jnp.zeros_like(l_ref)
    acc[...] = jnp.zeros_like(acc)

    def attend(slots, seg, masked=False):
        keys = [[kv[slot, seg, 0, g] for slot in slots] for g in range(groups)]
        values = [[kv[slot, seg, 1, g].T for slot in slots] for g in range(groups)]
        if masked:
            key = lax.broadcasted_iota(jnp.int32, (rows, rows), 0)
            tok = lax.broadcasted_iota(jnp.int32, (rows, rows), 1)
            allowed = key <= tok

        def scores(h):
            q = qrot[seg, h]
            parts = [
                lax.dot_general(k, q, (((1,), (1,)), ((), ())), preferred_element_type=F32)
                for k in keys[h // per]
            ]
            return [jnp.where(allowed, s, MASKED) for s in parts] if masked else parts

        def gather(h, weights, alpha):
            parts = [
                jnp.dot(vt, p, preferred_element_type=F32)
                for vt, p in zip(values[h // per], weights)
            ]
            acc[h] = acc[h] * alpha + functools.reduce(jnp.add, parts)

        ahead, behind = scores(0), None
        for h in range(groups * per):
            now = ahead
            if h + 1 < groups * per:
                ahead = scores(h + 1)
            m_old = m_ref[h]
            m_new = jnp.maximum(
                m_old, jnp.max(functools.reduce(jnp.maximum, now), axis=0, keepdims=True)
            )
            alpha = jnp.exp2((m_old - m_new) * SCALE2)
            weights = [jnp.exp2((s - m_new) * SCALE2) for s in now]
            m_ref[h] = m_new
            l_ref[h] = l_ref[h] * alpha + jnp.sum(
                functools.reduce(jnp.add, weights), axis=0, keepdims=True
            )
            if behind is not None:
                gather(*behind)
            behind = (h, [p.astype(BF16) for p in weights], alpha)
        gather(*behind)

    def first(seg, _):
        attend((me,), seg)
        return 0

    lax.fori_loop(0, 2, first, 0)
    attend((me,), 2, True)

    def step(t, _):
        def of_seg(seg, _):
            for way in range(2):
                slot = lax.rem(me + (n - t if way == 0 else t), n)
                for side in range(2):
                    ring(way, slot, seg, side).wait_recv()
                    if side == way:
                        ring(way, slot, seg, side).start()
                    else:
                        @pl.when(t < half - 1)
                        def _():
                            ring(way, slot, seg, side).start()

            up, down = lax.rem(me + n - t, n), lax.rem(me + t, n)
            up_counts = (seg < 2) | (up < me)
            down_counts = (seg < 2) | (down < me)

            @pl.when(up_counts & down_counts)
            def _():
                attend((up, down), seg)

            @pl.when(up_counts != down_counts)
            def _():
                attend((jnp.where(up_counts, up, down),), seg)

            return 0

        lax.fori_loop(0, 3, of_seg, 0)
        return 0

    lax.fori_loop(1, half, step, 0)

    far = lax.rem(me + half, n)

    def last(seg, _):
        for side in range(2):
            ring(side, far, seg, side).wait_recv()

        @pl.when((seg < 2) | (far < me))
        def _():
            attend((far,), seg)

        return 0

    lax.fori_loop(0, 3, last, 0)

    at = pl.ds(pl.multiple_of(me * PAGE, PAGE), PAGE)

    def page(s, _):
        def find(j, found):
            return jnp.maximum(found, jnp.where(table_ref[j * n + me] == s, j, 0))

        source = lax.fori_loop(0, n, find, 0)
        for g in range(groups):
            pk_ref[g, s] = kv[source, 1, 0, g, at, :]
            pv_ref[g, s] = kv[source, 1, 1, g, at, :]
        return 0

    lax.fori_loop(0, n, page, 0)

    for h in range(groups * per):
        out_ref[:, h * HEAD : (h + 1) * HEAD] = (acc[h] / l_ref[h]).T.astype(BF16)

    def drain(t, _):
        for way in range(2):
            slot = lax.rem(me + (n - t if way == 0 else t), n)
            for seg in range(3):
                for side in range(2):
                    if side == way:
                        ring(way, slot, seg, side).wait_send()
                    else:
                        @pl.when(t < half - 1)
                        def _():
                            ring(way, slot, seg, side).wait_send()
        return 0

    lax.fori_loop(0, half, drain, 0)


def shards(queries, current_keys, current_values, stored_keys, stored_values, remap_table, block_table, *, n):
    rows = queries.shape[0]
    groups = current_keys.shape[1] // HEAD
    heads = queries.shape[1] // HEAD
    d = np.arange(HEAD // 2, dtype=np.float32)
    freq = (np.float32(ROPE_BASE) ** (np.float32(-2.0) * d / np.float32(HEAD))).astype(np.float32)
    freq = jnp.asarray(np.concatenate([freq, freq])[None, :])
    flat = lambda a: a.reshape(rows, -1)
    smem = pl.BlockSpec(memory_space=pltpu.SMEM)
    vmem = pl.BlockSpec(memory_space=pltpu.VMEM)
    hbm = pl.BlockSpec(memory_space=pl.ANY)
    attended, pk, pv = pl.pallas_call(
        functools.partial(kernel, n, groups, heads // groups),
        out_shape=(
            jax.ShapeDtypeStruct(queries.shape, BF16),
            jax.ShapeDtypeStruct((groups, n, PAGE, HEAD), BF16),
            jax.ShapeDtypeStruct((groups, n, PAGE, HEAD), BF16),
        ),
        in_specs=[smem, smem, vmem, vmem, hbm, hbm, hbm, hbm],
        out_specs=(vmem, vmem, vmem),
        scratch_shapes=[
            pltpu.VMEM((n, 3, 2, groups, rows, HEAD), BF16),
            pltpu.VMEM((3, heads, rows, HEAD), BF16),
            pltpu.VMEM((heads, HEAD, rows), F32),
            pltpu.VMEM((heads, 1, rows), F32),
            pltpu.VMEM((heads, 1, rows), F32),
            pltpu.SemaphoreType.DMA((3, 2, groups)),
            pltpu.SemaphoreType.DMA((2, n, 3, 2)),
            pltpu.SemaphoreType.DMA((n, 3, 2)),
        ],
        compiler_params=pltpu.CompilerParams(
            collective_id=0, has_side_effects=True, vmem_limit_bytes=60 * 1024 * 1024
        ),
    )(
        block_table, remap_table, freq, queries,
        flat(stored_keys), flat(stored_values), current_keys, current_values,
    )
    return attended, pk.reshape(groups, n, -1), pv.reshape(groups, n, -1)


def solution(mesh):
    both = ("groups", "seq")
    in_specs = (
        P(both, "head"), P(both, "head"), P(both, "head"),
        P(both, None, "head"), P(both, None, "head"),
        P(None, both), P("groups"),
    )
    out_specs = (P(both, "head"), P("head", both, None), P("head", both, None))
    return jax.shard_map(
        functools.partial(shards, n=mesh.shape["seq"]),
        mesh=mesh, in_specs=in_specs, out_specs=out_specs, check_vma=False,
    )
```

time: 457 us -> 158 us (0.35)
  the two profiles are of different devices: /device:TPU:1988 before, /device:TPU:86 now
where the time goes in v1:
time: 158 us
  Pallas kernels  150 us (95%)
  local copies, waits for them, and re-layouts  6.99 us (4%)
    pallas_call x1, Pallas kernels, shards(): pl.pallas_call(functools.partial(kernel, n, groups, heads // groups), out...  150 us
    unnamed x7, local copies, waits for them, and re-layouts  4.62 us

profile of v1, /device:TPU:86, one launch (start us, length us, event | category | flops | bytes accessed | tf_op | source)
XLA Modules:
  0.0 157.6 jit_solution(9752833806874788289)
XLA Ops:
  0.6 0.0 copy-start
  0.6 1.7 %copy.11 = bf16[32,8,2,256]{3,1,2,0:T(8,128)(2,1)} copy(bf16[32,8,2,256]{3,2,1,0:T(2,128)(2,1)} %bitcast.10) | data formatting | bytes 524288
  2.4 0.0 copy-done
  2.4 0.7 copy.12
  3.1 149.9 %shard_map.103 = (bf16[256,1792]{1,0:T(8,128)(2,1)}, bf16[2,16,16,128]{3,2,1,0:T(8,128)(2,1)}, bf16[2,16,16,128]{3,2,1,0:T(8,128)(2,1)}) custom-call(s32[256]{0:T(256)} %table_ref.1, s32[3,4]{1,0:T(4,128)} %remap_ref.1, f32[1,128]{1,0:T(1,128)} %constant.2.clone.freq_ref, bf16[256,1792]{1,0:T(8,128)(2,1)} %q_ref.1, bf16[256,512]{1,0:T(8,128)(2,1)} %bitcast.8, ...), custom_call_target="tpu_custom_call" | custom-call | tf_op jit(solution)/shard_map/pallas_call | solution.py:235
  153.0 0.0 copy-start.1
  153.0 1.7 %reshape.20 = bf16[2,16,2048]{2,1,0:T(8,128)(2,1)} reshape(bf16[2,16,16,128]{3,2,1,0:T(8,128)(2,1)} %get-tuple-element.7) | data formatting | bytes 262144 | tf_op jit(solution)/shard_map/reshape | solution.py:261
  154.7 0.0 copy-done.1
  154.7 0.7 reshape.21
  155.4 2.2 %copy.14 = bf16[256,1792]{1,0:T(8,128)(2,1)} copy(bf16[256,1792]{1,0:T(8,128)(2,1)} %get-tuple-element.12) | data formatting | bytes 1835008
Async XLA Ops:
  0.6 1.7 %copy-start = (bf16[256,2,256]{2,1,0:T(2,128)(2,1)S(1)}, bf16[256,2,256]{2,1,0:T(2,128)(2,1)}, u32[]{:S(2)}) copy-start(bf16[256,2,256]{2,1,0:T(2,128)(2,1)} %param.12) | copy-start | bytes 786436
  153.0 1.7 %copy-start.1 = (bf16[2,16,16,128]{3,2,1,0:T(8,128)(2,1)S(1)}, bf16[2,16,16,128]{3,2,1,0:T(8,128)(2,1)}, u32[]{:S(2)}) copy-start(bf16[2,16,16,128]{3,2,1,0:T(8,128)(2,1)} %get-tuple-element.8) | copy-start | bytes 393220

commit v2 on v1

v2 whole, which is shorter than its diff:
```python
import functools

import jax
import jax.numpy as jnp
import numpy as np
from jax import lax
from jax.experimental import pallas as pl
from jax.experimental.pallas import tpu as pltpu
from jax.sharding import PartitionSpec as P

HEAD = 128
PAGE = 16
QBLK = 64
ROPE_BASE = 1000000.0
MASKED = -1e30
MESH = pl.DeviceIdType.MESH
F32 = jnp.float32
BF16 = jnp.bfloat16
SCALE2 = float(HEAD**-0.5 * np.log2(np.e))


def kernel(
    n, groups, per,
    table_ref, remap_ref, freq_ref, q_hbm, sk_hbm, sv_hbm, ck_hbm, cv_hbm,
    out_ref, pk_ref, pv_ref,
    kv, q_ref, raw, qrot, acc, m_ref, l_ref, pages, turned_pages, source_ref,
    own_sem, raw_sem, q_sem, send_sem, recv_sem,
):
    me = lax.axis_index("seq")
    half = n // 2
    rows = q_ref.shape[0]
    heads = groups * per
    right, left = lax.rem(me + 1, n), lax.rem(me + n - 1, n)

    def current(side, g):
        return pltpu.make_async_copy(
            (ck_hbm, cv_hbm)[side].at[:, pl.ds(g * HEAD, HEAD)], kv.at[me, 2, side, g], own_sem.at[side, g]
        )

    def stored(side):
        return pltpu.make_async_copy((sk_hbm, sv_hbm)[side], raw.at[side], raw_sem.at[side])

    all_queries = pltpu.make_async_copy(q_hbm, q_ref, q_sem)

    barrier = pltpu.get_barrier_semaphore()
    for neighbour in (left, right):
        pl.semaphore_signal(barrier, inc=1, device_id={"seq": neighbour}, device_id_type=MESH)
    for side in range(2):
        for g in range(groups):
            current(side, g).start()
    for side in range(2):
        stored(side).start()
    all_queries.start()

    def ring(way, slot, seg, side):
        unit = kv.at[slot, seg, side]
        return pltpu.make_async_remote_copy(
            src_ref=unit,
            dst_ref=unit,
            send_sem=send_sem.at[way, slot, seg, side],
            recv_sem=recv_sem.at[slot, seg, side],
            device_id={"seq": (right, left)[way]},
            device_id_type=MESH,
        )

    def wanted(way, slot, seg, to):
        return (seg < 2) | ((slot < to) if way == 0 else (slot + 1 < half))

    def goes_on(way, t, slot, seg, side):
        if side == way:
            return True
        near = t < half - 1
        return near | ((seg == 2) & (slot == half - 1)) if way == 0 else near

    def send_own(seg):
        for side in range(2):
            for way in range(2):
                @pl.when(wanted(way, me, seg, right))
                def _():
                    ring(way, me, seg, side).start()

    for side in range(2):
        for g in range(groups):
            current(side, g).wait()
    pl.semaphore_wait(barrier, 2)
    send_own(2)

    for side in range(2):
        stored(side).wait()
        both = raw[side].astype(F32)
        for seg in range(2):
            for g in range(groups):
                kv[me, seg, side, g] = both[:, seg, g * HEAD : (g + 1) * HEAD].astype(BF16)

    def find(s, _):
        source_ref[s] = lax.fori_loop(
            0, n, lambda j, found: jnp.maximum(found, jnp.where(table_ref[j * n + me] == s, j, 0)), 0
        )
        return 0

    lax.fori_loop(0, n, find, 0)
    for seg in (1, 0):
        send_own(seg)

    lanes = lax.broadcasted_iota(jnp.int32, (QBLK, HEAD), 1)
    rising = lax.broadcasted_iota(jnp.int32, (QBLK, HEAD), 0)
    freq = freq_ref[...]
    all_queries.wait()

    def rotate(step, _):
        kind = step // (rows // QBLK)
        blk = lax.rem(step, rows // QBLK)
        angle = (rising + remap_ref[kind, blk]).astype(F32) * freq
        cos = jnp.cos(angle)
        sin = jnp.sin(angle)
        sin = jnp.where(lanes < HEAD // 2, -sin, sin)
        at = pl.ds(pl.multiple_of(blk * QBLK, QBLK), QBLK)
        for h in range(heads):
            x = q_ref[at, h * HEAD : (h + 1) * HEAD].astype(F32)
            turned = x * cos + pltpu.roll(x, HEAD // 2, 1) * sin
            qrot[2 - kind, h, at, :] = turned.astype(BF16)
        return 0

    lax.fori_loop(0, 3 * (rows // QBLK), rotate, 0)

    m_ref[...] = jnp.full_like(m_ref, MASKED)
    l_ref[...] = jnp.zeros_like(l_ref)
    acc[...] = jnp.zeros_like(acc)

    def attend(slots, seg, masked=False, finish=False):
        keys = [[kv[slot, seg, 0, g] for slot in slots] for g in range(groups)]
        values = [[kv[slot, seg, 1, g].T for slot in slots] for g in range(groups)]
        if masked:
            key = lax.broadcasted_iota(jnp.int32, (rows, rows), 0)
            tok = lax.broadcasted_iota(jnp.int32, (rows, rows), 1)
            allowed = key <= tok

        def scores(h):
            q = qrot[seg, h]
            parts = [
                lax.dot_general(k, q, (((1,), (1,)), ((), ())), preferred_element_type=F32)
                for k in keys[h // per]
            ]
            return [jnp.where(allowed, s, MASKED) for s in parts] if masked else parts

        def gather(h, weights, alpha):
            parts = [
                jnp.dot(vt, p, preferred_element_type=F32)
                for vt, p in zip(values[h // per], weights)
            ]
            total = acc[h] * alpha + functools.reduce(jnp.add, parts)
            if finish:
                out_ref[:, h * HEAD : (h + 1) * HEAD] = (total / l_ref[h]).T.astype(BF16)
            else:
                acc[h] = total

        ahead, behind = scores(0), None
        for h in range(heads):
            now = ahead
            if h + 1 < heads:
                ahead = scores(h + 1)
            m_old = m_ref[h]
            m_new = jnp.maximum(
                m_old, jnp.max(functools.reduce(jnp.maximum, now), axis=0, keepdims=True)
            )
            alpha = jnp.exp2((m_old - m_new) * SCALE2)
            weights = [jnp.exp2((s - m_new) * SCALE2) for s in now]
            m_ref[h] = m_new
            l_ref[h] = l_ref[h] * alpha + jnp.sum(
                functools.reduce(jnp.add, weights), axis=0, keepdims=True
            )
            if behind is not None:
                gather(*behind)
            behind = (h, [p.astype(BF16) for p in weights], alpha)
        gather(*behind)

    page_rows = pl.ds(pl.multiple_of(me * PAGE, PAGE), PAGE)

    def keep_page(slot):
        for side in range(2):
            for g in range(groups):
                pages[slot, side, g] = kv[slot, 1, side, g, page_rows, :]

    def first(seg, _):
        attend((me,), seg)
        return 0

    keep_page(me)
    lax.fori_loop(0, 2, first, 0)
    attend((me,), 2, True)

    def step(t, _):
        up, down = lax.rem(me + n - t, n), lax.rem(me + t, n)

        def of_seg(i, _):
            seg = 2 - i
            for side in range(2):
                for way in range(2):
                    slot = (up, down)[way]

                    @pl.when(wanted(way, slot, seg, me))
                    def _():
                        ring(way, slot, seg, side).wait_recv()

                    @pl.when(wanted(way, slot, seg, right) & goes_on(way, t, slot, seg, side))
                    def _():
                        ring(way, slot, seg, side).start()

            @pl.when(seg == 1)
            def _():
                keep_page(up)
                keep_page(down)

            up_counts = (seg < 2) | (up < me)
            down_counts = (seg < 2) | (down < me)

            @pl.when(up_counts & down_counts)
            def _():
                attend((up, down), seg)

            @pl.when(up_counts != down_counts)
            def _():
                attend((jnp.where(up_counts, up, down),), seg)

            return 0

        lax.fori_loop(0, 3, of_seg, 0)
        return 0

    lax.fori_loop(1, half, step, 0)

    far = lax.rem(me + half, n)

    def last(i, _):
        seg = 2 - i

        @pl.when((seg < 2) | (far < me))
        def _():
            for side in range(2):
                ring(side, far, seg, side).wait_recv()
            attend((far,), seg)

        return 0

    lax.fori_loop(0, 2, last, 0)
    keep_page(far)

    def place(s, _):
        source = source_ref[s]
        at = pl.ds(pl.multiple_of(s * PAGE, PAGE), PAGE)
        for side in range(2):
            for g in range(groups):
                turned_pages[side, g, at, :] = pages[source, side, g].astype(F32)
        return 0

    lax.fori_loop(0, n, place, 0)
    for side, ref in enumerate((pk_ref, pv_ref)):
        for g in range(groups):
            for t in range(PAGE):
                ref[g, :, t * HEAD : (t + 1) * HEAD] = turned_pages[
                    side, g, pl.ds(t, n, stride=PAGE), :
                ].astype(BF16)

    for side in range(2):
        ring(side, far, 0, side).wait_recv()
    attend((far,), 0, finish=True)

    def drain(t, _):
        def of_seg(seg, _):
            for way in range(2):
                slot = lax.rem(me + (n - t if way == 0 else t), n)
                for side in range(2):
                    @pl.when(wanted(way, slot, seg, right) & goes_on(way, t, slot, seg, side))
                    def _():
                        ring(way, slot, seg, side).wait_send()
            return 0

        lax.fori_loop(0, 3, of_seg, 0)
        return 0

    lax.fori_loop(0, half, drain, 0)


def shards(queries, current_keys, current_values, stored_keys, stored_values, remap_table, block_table, *, n):
    rows = queries.shape[0]
    groups = current_keys.shape[1] // HEAD
    heads = queries.shape[1] // HEAD
    d = np.arange(HEAD // 2, dtype=np.float32)
    freq = (np.float32(ROPE_BASE) ** (np.float32(-2.0) * d / np.float32(HEAD))).astype(np.float32)
    freq = jnp.asarray(np.concatenate([freq, freq])[None, :])
    smem = pl.BlockSpec(memory_space=pltpu.SMEM)
    vmem = pl.BlockSpec(memory_space=pltpu.VMEM)
    hbm = pl.BlockSpec(memory_space=pltpu.HBM)
    paged = pltpu.VMEM((groups, n, PAGE * HEAD), BF16)
    return pl.pallas_call(
        functools.partial(kernel, n, groups, heads // groups),
        out_shape=(pltpu.VMEM(queries.shape, BF16), paged, paged),
        in_specs=[smem, smem, vmem, hbm, hbm, hbm, hbm, hbm],
        out_specs=(vmem, vmem, vmem),
        scratch_shapes=[
            pltpu.VMEM((n, 3, 2, groups, rows, HEAD), BF16),
            pltpu.VMEM(queries.shape, BF16),
            pltpu.VMEM((2, *stored_keys.shape), BF16),
            pltpu.VMEM((3, heads, rows, HEAD), BF16),
            pltpu.VMEM((heads, HEAD, rows), F32),
            pltpu.VMEM((heads, 1, rows), F32),
            pltpu.VMEM((heads, 1, rows), F32),
            pltpu.VMEM((n, 2, groups, PAGE, HEAD), BF16),
            pltpu.VMEM((2, groups, n * PAGE, HEAD), F32),
            pltpu.SMEM((n,), jnp.int32),
            pltpu.SemaphoreType.DMA((2, groups)),
            pltpu.SemaphoreType.DMA((2,)),
            pltpu.SemaphoreType.DMA,
            pltpu.SemaphoreType.DMA((2, n, 3, 2)),
            pltpu.SemaphoreType.DMA((n, 3, 2)),
        ],
        compiler_params=pltpu.CompilerParams(
            collective_id=0, has_side_effects=True, vmem_limit_bytes=58 * 1024 * 1024
        ),
    )(
        block_table, remap_table, freq, queries,
        stored_keys, stored_values, current_keys, current_values,
    )


def solution(mesh):
    both = ("groups", "seq")
    in_specs = (
        P(both, "head"), P(both, "head"), P(both, "head"),
        P(both, None, "head"), P(both, None, "head"),
        P(None, both), P("groups"),
    )
    out_specs = (P(both, "head"), P("head", both, None), P("head", both, None))
    return jax.shard_map(
        functools.partial(shards, n=mesh.shape["seq"]),
        mesh=mesh, in_specs=in_specs, out_specs=out_specs, check_vma=False,
    )
```

time: 158 us -> 145 us (0.918)
  Pallas kernels: 150 us -> 142 us
  local copies, waits for them, and re-layouts: 6.99 us -> 2.23 us
    pallas_call x1, Pallas kernels: 150 us -> 142 us  [shards(): pl.pallas_call(functools.partial(kernel, n, groups, heads // groups), out...]
    unnamed x7 -> x3, local copies, waits for them, and re-layouts: 4.62 us -> 2.23 us
    reshape x2 -> x0, local copies, waits for them, and re-layouts: 2.37 us -> none  [shards(): return (attended, pk.reshape(groups, n, -1), pv.reshape(groups, n, -1))]
where the time goes in v2:
time: 145 us; the launch traced here: 144 us
  Pallas kernels  142 us (98%)
  local copies, waits for them, and re-layouts  2.23 us (2%)
    pallas_call x1, Pallas kernels, shards(): pl.pallas_call(functools.partial(kernel, n, groups, heads // groups), out...  142 us

profile of v2, /device:TPU:86, one launch (start us, length us, event | category | flops | bytes accessed | tf_op | source)
XLA Modules:
  0.0 144.4 jit_solution(6597518889935005531)
XLA Ops:
  0.6 141.5 %shard_map.103 = (bf16[256,1792]{1,0:T(8,128)(2,1)S(1)}, bf16[2,16,2048]{2,1,0:T(8,128)(2,1)S(1)}, bf16[2,16,2048]{2,1,0:T(8,128)(2,1)S(1)}) custom-call(s32[256]{0:T(256)} %table_ref.1, s32[3,4]{1,0:T(4,128)} %remap_ref.1, f32[1,128]{1,0:T(1,128)} %constant.2.clone.freq_ref, bf16[256,1792]{1,0:T(8,128)(2,1)} %q_hbm.1, bf16[256,2,256]{2,1,0:T(2,128)(2,1)} %sk_hbm.1, ...), custom_call_target="tpu_custom_call" | custom-call | tf_op jit(solution)/shard_map/pallas_call | solution.py:295
  142.2 0.9 copy.14
  143.1 0.7 copy.15
  143.8 0.7 copy.16

commit v3 on v2

--- a/solution.py
+++ b/solution.py
@@ -21,10 +21,10 @@
 
 def kernel(
     n, groups, per,
-    table_ref, remap_ref, freq_ref, q_hbm, sk_hbm, sv_hbm, ck_hbm, cv_hbm,
+    table_hbm, remap_hbm, freq_hbm, q_hbm, sk_hbm, sv_hbm, ck_hbm, cv_hbm,
     out_ref, pk_ref, pv_ref,
-    kv, q_ref, raw, qrot, acc, m_ref, l_ref, pages, turned_pages, source_ref,
-    own_sem, raw_sem, q_sem, send_sem, recv_sem,
+    table_ref, remap_ref, freq_ref, kv, q_ref, raw, qrot, acc, m_ref, l_ref, pages, turned_pages, source_ref,
+    small_sem, own_sem, raw_sem, q_sem, send_sem, recv_sem, far_send, far_recv,
 ):
     me = lax.axis_index("seq")
     half = n // 2
@@ -41,6 +41,12 @@
         return pltpu.make_async_copy((sk_hbm, sv_hbm)[side], raw.at[side], raw_sem.at[side])
 
     all_queries = pltpu.make_async_copy(q_hbm, q_ref, q_sem)
+    small = [
+        pltpu.make_async_copy(src, dst, small_sem.at[i])
+        for i, (src, dst) in enumerate(
+            ((table_hbm, table_ref), (remap_hbm, remap_ref), (freq_hbm, freq_ref))
+        )
+    ]
 
     barrier = pltpu.get_barrier_semaphore()
     for neighbour in (left, right):
@@ -50,6 +56,8 @@
             current(side, g).start()
     for side in range(2):
         stored(side).start()
+    for copy in small:
+        copy.start()
     all_queries.start()
 
     def ring(way, slot, seg, side):
@@ -63,14 +71,28 @@
             device_id_type=MESH,
         )
 
+    def part(way, slot, side, g):
+        unit = kv.at[slot, 0, side, g]
+        return pltpu.make_async_remote_copy(
+            src_ref=unit,
+            dst_ref=unit,
+            send_sem=far_send.at[way, side, g],
+            recv_sem=far_recv.at[side, g],
+            device_id={"seq": (right, left)[way]},
+            device_id_type=MESH,
+        )
+
     def wanted(way, slot, seg, to):
         return (seg < 2) | ((slot < to) if way == 0 else (slot + 1 < half))
 
-    def goes_on(way, t, slot, seg, side):
-        if side == way:
-            return True
-        near = t < half - 1
-        return near | ((seg == 2) & (slot == half - 1)) if way == 0 else near
+    def from_left(to, seg, side):
+        if side == 0:
+            return (to < half) | (to >= n - 2)
+        return (to < half - 2) | ((to == n - 1) & (seg == 2))
+
+    def goes_on(way, t, seg, side):
+        last = from_left(right, seg, side) if way == 0 else jnp.logical_not(from_left(left, seg, side))
+        return (t < half - 1) | last
 
     def send_own(seg):
         for side in range(2):
@@ -91,6 +113,9 @@
         for seg in range(2):
             for g in range(groups):
                 kv[me, seg, side, g] = both[:, seg, g * HEAD : (g + 1) * HEAD].astype(BF16)
+
+    for copy in small:
+        copy.wait()
 
     def find(s, _):
         source_ref[s] = lax.fori_loop(
@@ -127,9 +152,11 @@
     l_ref[...] = jnp.zeros_like(l_ref)
     acc[...] = jnp.zeros_like(acc)
 
-    def attend(slots, seg, masked=False, finish=False):
-        keys = [[kv[slot, seg, 0, g] for slot in slots] for g in range(groups)]
-        values = [[kv[slot, seg, 1, g].T for slot in slots] for g in range(groups)]
+    def attend(slots, seg, masked=False, finish=False, only=None):
+        chosen = range(groups) if only is None else (only,)
+        hs = range(chosen[0] * per, (chosen[-1] + 1) * per)
+        keys = {g: [kv[slot, seg, 0, g] for slot in slots] for g in chosen}
+        values = {g: [kv[slot, seg, 1, g].T for slot in slots] for g in chosen}
         if masked:
             key = lax.broadcasted_iota(jnp.int32, (rows, rows), 0)
             tok = lax.broadcasted_iota(jnp.int32, (rows, rows), 1)
@@ -154,10 +181,10 @@
             else:
                 acc[h] = total
 
-        ahead, behind = scores(0), None
-        for h in range(heads):
+        ahead, behind = scores(hs[0]), None
+        for h in hs:
             now = ahead
-            if h + 1 < heads:
+            if h + 1 in hs:
                 ahead = scores(h + 1)
             m_old = m_ref[h]
             m_new = jnp.maximum(
@@ -202,9 +229,17 @@
                     def _():
                         ring(way, slot, seg, side).wait_recv()
 
-                    @pl.when(wanted(way, slot, seg, right) & goes_on(way, t, slot, seg, side))
+                    sends = wanted(way, slot, seg, right) & goes_on(way, t, seg, side)
+                    split = (t == half - 1) & (seg == 0)
+
+                    @pl.when(sends & jnp.logical_not(split))
                     def _():
                         ring(way, slot, seg, side).start()
+
+                    @pl.when(sends & split)
+                    def _():
+                        for g in range(groups):
+                            part(way, slot, side, g).start()
 
             @pl.when(seg == 1)
             def _():
@@ -261,18 +296,27 @@
                     side, g, pl.ds(t, n, stride=PAGE), :
                 ].astype(BF16)
 
-    for side in range(2):
-        ring(side, far, 0, side).wait_recv()
-    attend((far,), 0, finish=True)
+    for g in range(groups):
+        for side in range(2):
+            part(side, far, side, g).wait_recv()
+        attend((far,), 0, finish=True, only=g)
 
     def drain(t, _):
         def of_seg(seg, _):
             for way in range(2):
                 slot = lax.rem(me + (n - t if way == 0 else t), n)
                 for side in range(2):
-                    @pl.when(wanted(way, slot, seg, right) & goes_on(way, t, slot, seg, side))
+                    sends = wanted(way, slot, seg, right) & goes_on(way, t, seg, side)
+                    split = (t == half - 1) & (seg == 0)
+
+                    @pl.when(sends & jnp.logical_not(split))
                     def _():
                         ring(way, slot, seg, side).wait_send()
+
+                    @pl.when(sends & split)
+                    def _():
+                        for g in range(groups):
+                            part(way, slot, side, g).wait_send()
             return 0
 
         lax.fori_loop(0, 3, of_seg, 0)
@@ -288,16 +332,18 @@
     d = np.arange(HEAD // 2, dtype=np.float32)
     freq = (np.float32(ROPE_BASE) ** (np.float32(-2.0) * d / np.float32(HEAD))).astype(np.float32)
     freq = jnp.asarray(np.concatenate([freq, freq])[None, :])
-    smem = pl.BlockSpec(memory_space=pltpu.SMEM)
     vmem = pl.BlockSpec(memory_space=pltpu.VMEM)
     hbm = pl.BlockSpec(memory_space=pltpu.HBM)
     paged = pltpu.VMEM((groups, n, PAGE * HEAD), BF16)
     return pl.pallas_call(
         functools.partial(kernel, n, groups, heads // groups),
         out_shape=(pltpu.VMEM(queries.shape, BF16), paged, paged),
-        in_specs=[smem, smem, vmem, hbm, hbm, hbm, hbm, hbm],
+        in_specs=[hbm] * 8,
         out_specs=(vmem, vmem, vmem),
         scratch_shapes=[
+            pltpu.SMEM(block_table.shape, jnp.int32),
+            pltpu.SMEM(remap_table.shape, jnp.int32),
+            pltpu.VMEM(freq.shape, F32),
             pltpu.VMEM((n, 3, 2, groups, rows, HEAD), BF16),
             pltpu.VMEM(queries.shape, BF16),
             pltpu.VMEM((2, *stored_keys.shape), BF16),
@@ -308,11 +354,14 @@
             pltpu.VMEM((n, 2, groups, PAGE, HEAD), BF16),
             pltpu.VMEM((2, groups, n * PAGE, HEAD), F32),
             pltpu.SMEM((n,), jnp.int32),
+            pltpu.SemaphoreType.DMA((3,)),
             pltpu.SemaphoreType.DMA((2, groups)),
             pltpu.SemaphoreType.DMA((2,)),
             pltpu.SemaphoreType.DMA,
             pltpu.SemaphoreType.DMA((2, n, 3, 2)),
             pltpu.SemaphoreType.DMA((n, 3, 2)),
+            pltpu.SemaphoreType.DMA((2, 2, groups)),
+            pltpu.SemaphoreType.DMA((2, groups)),
         ],
         compiler_params=pltpu.CompilerParams(
             collective_id=0, has_side_effects=True, vmem_limit_bytes=58 * 1024 * 1024

time: 145 us -> 146 us (level)
    pallas_call x1, Pallas kernels: 142 us -> 143 us  [shards(): pl.pallas_call(functools.partial(kernel, n, groups, heads // groups), out...]
where the time goes in v3:
time: 146 us
  Pallas kernels  143 us (98%)
  local copies, waits for them, and re-layouts  2.23 us (2%)
    pallas_call x1, Pallas kernels, shards(): pl.pallas_call(functools.partial(kernel, n, groups, heads // groups), out...  143 us

profile of v3, /device:TPU:86, one launch (start us, length us, event | category | flops | bytes accessed | tf_op | source)
XLA Modules:
  0.0 146.0 jit_solution(9825324584289763677)
XLA Ops:
  0.6 143.1 %shard_map.103 = (bf16[256,1792]{1,0:T(8,128)(2,1)S(1)}, bf16[2,16,2048]{2,1,0:T(8,128)(2,1)S(1)}, bf16[2,16,2048]{2,1,0:T(8,128)(2,1)S(1)}) custom-call(s32[256]{0:T(256)} %table_hbm.1, s32[3,4]{1,0:T(4,128)} %remap_hbm.1, f32[1,128]{1,0:T(1,128)} %constant.2.clone.freq_hbm, bf16[256,1792]{1,0:T(8,128)(2,1)} %q_hbm.1, bf16[256,2,256]{2,1,0:T(2,128)(2,1)} %sk_hbm.1, ...), custom_call_target="tpu_custom_call" | custom-call | tf_op jit(solution)/shard_map/pallas_call | solution.py:338
  143.7 0.9 copy.14
  144.7 0.7 copy.15
  145.3 0.7 copy.16

commit v4 on v3

--- a/solution.py
+++ b/solution.py
@@ -60,26 +60,22 @@
         copy.start()
     all_queries.start()
 
-    def ring(way, slot, seg, side):
-        unit = kv.at[slot, seg, side]
+    def send(unit, way, send_sem, recv_sem):
         return pltpu.make_async_remote_copy(
             src_ref=unit,
             dst_ref=unit,
-            send_sem=send_sem.at[way, slot, seg, side],
-            recv_sem=recv_sem.at[slot, seg, side],
+            send_sem=send_sem,
+            recv_sem=recv_sem,
             device_id={"seq": (right, left)[way]},
             device_id_type=MESH,
         )
 
-    def part(way, slot, side, g):
-        unit = kv.at[slot, 0, side, g]
-        return pltpu.make_async_remote_copy(
-            src_ref=unit,
-            dst_ref=unit,
-            send_sem=far_send.at[way, side, g],
-            recv_sem=far_recv.at[side, g],
-            device_id={"seq": (right, left)[way]},
-            device_id_type=MESH,
+    def ring(way, slot, seg):
+        return send(kv.at[slot, seg], way, send_sem.at[way, slot, seg], recv_sem.at[slot, seg])
+
+    def part(way, slot, seg, side, g):
+        return send(
+            kv.at[slot, seg, side, g], way, far_send.at[way, seg, side, g], far_recv.at[seg, side, g]
         )
 
     def wanted(way, slot, seg, to):
@@ -88,18 +84,16 @@
     def from_left(to, seg, side):
         if side == 0:
             return (to < half) | (to >= n - 2)
-        return (to < half - 2) | ((to == n - 1) & (seg == 2))
-
-    def goes_on(way, t, seg, side):
-        last = from_left(right, seg, side) if way == 0 else jnp.logical_not(from_left(left, seg, side))
-        return (t < half - 1) | last
+        return (to < half - 2) | ((to == n - 1) & (seg != 1))
+
+    def last_hop(way, seg, side):
+        return from_left(right, seg, side) if way == 0 else jnp.logical_not(from_left(left, seg, side))
 
     def send_own(seg):
-        for side in range(2):
-            for way in range(2):
-                @pl.when(wanted(way, me, seg, right))
-                def _():
-                    ring(way, me, seg, side).start()
+        for way in range(2):
+            @pl.when(wanted(way, me, seg, right))
+            def _():
+                ring(way, me, seg).start()
 
     for side in range(2):
         for g in range(groups):
@@ -221,25 +215,24 @@
 
         def of_seg(i, _):
             seg = 2 - i
-            for side in range(2):
-                for way in range(2):
-                    slot = (up, down)[way]
-
-                    @pl.when(wanted(way, slot, seg, me))
-                    def _():
-                        ring(way, slot, seg, side).wait_recv()
-
-                    sends = wanted(way, slot, seg, right) & goes_on(way, t, seg, side)
-                    split = (t == half - 1) & (seg == 0)
-
-                    @pl.when(sends & jnp.logical_not(split))
-                    def _():
-                        ring(way, slot, seg, side).start()
-
-                    @pl.when(sends & split)
+            for way in range(2):
+                slot = (up, down)[way]
+
+                @pl.when(wanted(way, slot, seg, me))
+                def _():
+                    ring(way, slot, seg).wait_recv()
+
+                sends = wanted(way, slot, seg, right)
+
+                @pl.when(sends & (t < half - 1))
+                def _():
+                    ring(way, slot, seg).start()
+
+                for side in range(2):
+                    @pl.when(sends & (t == half - 1) & last_hop(way, seg, side))
                     def _():
                         for g in range(groups):
-                            part(way, slot, side, g).start()
+                            part(way, slot, seg, side, g).start()
 
             @pl.when(seg == 1)
             def _():
@@ -272,7 +265,8 @@
         @pl.when((seg < 2) | (far < me))
         def _():
             for side in range(2):
-                ring(side, far, seg, side).wait_recv()
+                for g in range(groups):
+                    part(0, far, seg, side, g).wait_recv()
             attend((far,), seg)
 
         return 0
@@ -298,31 +292,41 @@
 
     for g in range(groups):
         for side in range(2):
-            part(side, far, side, g).wait_recv()
+            part(0, far, 0, side, g).wait_recv()
         attend((far,), 0, finish=True, only=g)
 
     def drain(t, _):
         def of_seg(seg, _):
             for way in range(2):
                 slot = lax.rem(me + (n - t if way == 0 else t), n)
+                sends = wanted(way, slot, seg, right)
+
+                @pl.when(sends & (t < half - 1))
+                def _():
+                    ring(way, slot, seg).wait_send()
+
                 for side in range(2):
-                    sends = wanted(way, slot, seg, right) & goes_on(way, t, seg, side)
-                    split = (t == half - 1) & (seg == 0)
-
-                    @pl.when(sends & jnp.logical_not(split))
-                    def _():
-                        ring(way, slot, seg, side).wait_send()
-
-                    @pl.when(sends & split)
+                    @pl.when(sends & (t == half - 1) & last_hop(way, seg, side))
                     def _():
                         for g in range(groups):
-                            part(way, slot, side, g).wait_send()
+                            part(way, slot, seg, side, g).wait_send()
             return 0
 
         lax.fori_loop(0, 3, of_seg, 0)
         return 0
 
     lax.fori_loop(0, half, drain, 0)
+
+
+def finish_kernel(a_ref, k_ref, v_ref, a_out, k_out, v_out, sem):
+    copies = [
+        pltpu.make_async_copy(src, dst, sem.at[i])
+        for i, (src, dst) in enumerate(((a_ref, a_out), (k_ref, k_out), (v_ref, v_out)))
+    ]
+    for copy in copies:
+        copy.start()
+    for copy in copies:
+        copy.wait()
 
 
 def shards(queries, current_keys, current_values, stored_keys, stored_values, remap_table, block_table, *, n):
@@ -335,7 +339,7 @@
     vmem = pl.BlockSpec(memory_space=pltpu.VMEM)
     hbm = pl.BlockSpec(memory_space=pltpu.HBM)
     paged = pltpu.VMEM((groups, n, PAGE * HEAD), BF16)
-    return pl.pallas_call(
+    results = pl.pallas_call(
         functools.partial(kernel, n, groups, heads // groups),
         out_shape=(pltpu.VMEM(queries.shape, BF16), paged, paged),
         in_specs=[hbm] * 8,
@@ -358,10 +362,10 @@
             pltpu.SemaphoreType.DMA((2, groups)),
             pltpu.SemaphoreType.DMA((2,)),
             pltpu.SemaphoreType.DMA,
-            pltpu.SemaphoreType.DMA((2, n, 3, 2)),
-            pltpu.SemaphoreType.DMA((n, 3, 2)),
-            pltpu.SemaphoreType.DMA((2, 2, groups)),
-            pltpu.SemaphoreType.DMA((2, groups)),
+            pltpu.SemaphoreType.DMA((2, n, 3)),
+            pltpu.SemaphoreType.DMA((n, 3)),
+            pltpu.SemaphoreType.DMA((2, 3, 2, groups)),
+            pltpu.SemaphoreType.DMA((3, 2, groups)),
         ],
         compiler_params=pltpu.CompilerParams(
             collective_id=0, has_side_effects=True, vmem_limit_bytes=58 * 1024 * 1024
@@ -370,6 +374,14 @@
         block_table, remap_table, freq, queries,
         stored_keys, stored_values, current_keys, current_values,
     )
+    return pl.pallas_call(
+        finish_kernel,
+        out_shape=tuple(jax.ShapeDtypeStruct(r.shape, BF16) for r in results),
+        in_specs=[vmem] * 3,
+        out_specs=(hbm, hbm, hbm),
+        scratch_shapes=[pltpu.SemaphoreType.DMA((3,))],
+        compiler_params=pltpu.CompilerParams(vmem_limit_bytes=4 * 1024 * 1024),
+    )(*results)
 
 
 def solution(mesh):

time: 146 us -> 145 us (level)
  local copies, waits for them, and re-layouts: 2.23 us -> 0 us
    unnamed x3 -> x0, local copies, waits for them, and re-layouts: 2.23 us -> none
where the time goes in v4:
time: 145 us
  Pallas kernels  144 us (99%)
    pallas_call x1, Pallas kernels, shards(): pl.pallas_call(functools.partial(kernel, n, groups, heads // groups), out...  143 us

profile of v4, /device:TPU:86, one launch (start us, length us, event | category | flops | bytes accessed | tf_op | source)
XLA Modules:
  0.0 145.0 jit_solution(9287207884353608781)
XLA Ops:
  0.6 143.3 %shard_map.103 = (bf16[256,1792]{1,0:T(8,128)(2,1)S(1)}, bf16[2,16,2048]{2,1,0:T(8,128)(2,1)S(1)}, bf16[2,16,2048]{2,1,0:T(8,128)(2,1)S(1)}) custom-call(s32[256]{0:T(256)} %table_hbm.1, s32[3,4]{1,0:T(4,128)} %remap_hbm.1, f32[1,128]{1,0:T(1,128)} %constant.2.clone.freq_hbm, bf16[256,1792]{1,0:T(8,128)(2,1)} %q_hbm.1, bf16[256,2,256]{2,1,0:T(2,128)(2,1)} %sk_hbm.1, ...), custom_call_target="tpu_custom_call" | custom-call | tf_op jit(solution)/shard_map/pallas_call | solution.py:342
  144.0 1.0 shard_map.104

commit v5 on v4

--- a/solution.py
+++ b/solution.py
@@ -83,8 +83,8 @@
 
     def from_left(to, seg, side):
         if side == 0:
-            return (to < half) | (to >= n - 2)
-        return (to < half - 2) | ((to == n - 1) & (seg != 1))
+            return to >= n - 2
+        return (to == n - 1) & (seg != 1)
 
     def last_hop(way, seg, side):
         return from_left(right, seg, side) if way == 0 else jnp.logical_not(from_left(left, seg, side))

time: 145 us -> 141 us (0.972)
  the two profiles are of different devices: /device:TPU:86 before, /device:TPU:2006 now
where the time goes in v5:
time: 141 us
  Pallas kernels  140 us (99%)
    pallas_call x1, Pallas kernels, shards(): pl.pallas_call(functools.partial(kernel, n, groups, heads // groups), out...  139 us

profile of v5, /device:TPU:2006, one launch (start us, length us, event | category | flops | bytes accessed | tf_op | source)
XLA Modules:
  0.0 140.7 jit_solution(6784889787108098267)
XLA Ops:
  0.6 139.1 %shard_map.103 = (bf16[256,1792]{1,0:T(8,128)(2,1)S(1)}, bf16[2,16,2048]{2,1,0:T(8,128)(2,1)S(1)}, bf16[2,16,2048]{2,1,0:T(8,128)(2,1)S(1)}) custom-call(s32[256]{0:T(256)} %table_hbm.1, s32[3,4]{1,0:T(4,128)} %remap_hbm.1, f32[1,128]{1,0:T(1,128)} %constant.2.clone.freq_hbm, bf16[256,1792]{1,0:T(8,128)(2,1)} %q_hbm.1, bf16[256,2,256]{2,1,0:T(2,128)(2,1)} %sk_hbm.1, ...), custom_call_target="tpu_custom_call" | custom-call | tf_op jit(solution)/shard_map/pallas_call | solution.py:342
  139.7 1.0 shard_map.104

commit v6 on v5

--- a/solution.py
+++ b/solution.py
@@ -81,13 +81,15 @@
     def wanted(way, slot, seg, to):
         return (seg < 2) | ((slot < to) if way == 0 else (slot + 1 < half))
 
-    def from_left(to, seg, side):
+    def from_left(to, seg, side, g):
         if side == 0:
             return to >= n - 2
-        return (to == n - 1) & (seg != 1)
-
-    def last_hop(way, seg, side):
-        return from_left(right, seg, side) if way == 0 else jnp.logical_not(from_left(left, seg, side))
+        return (to == n - 1) & ((seg == 2) | (seg == 0) if g == 0 else (seg == 2))
+
+    def last_hop(way, seg, side, g):
+        if way == 0:
+            return from_left(right, seg, side, g)
+        return jnp.logical_not(from_left(left, seg, side, g))
 
     def send_own(seg):
         for way in range(2):
@@ -229,9 +231,9 @@
                     ring(way, slot, seg).start()
 
                 for side in range(2):
-                    @pl.when(sends & (t == half - 1) & last_hop(way, seg, side))
-                    def _():
-                        for g in range(groups):
+                    for g in reversed(range(groups)):
+                        @pl.when(sends & (t == half - 1) & last_hop(way, seg, side, g))
+                        def _():
                             part(way, slot, seg, side, g).start()
 
             @pl.when(seg == 1)
@@ -290,7 +292,7 @@
                     side, g, pl.ds(t, n, stride=PAGE), :
                 ].astype(BF16)
 
-    for g in range(groups):
+    for g in reversed(range(groups)):
         for side in range(2):
             part(0, far, 0, side, g).wait_recv()
         attend((far,), 0, finish=True, only=g)
@@ -306,9 +308,9 @@
                     ring(way, slot, seg).wait_send()
 
                 for side in range(2):
-                    @pl.when(sends & (t == half - 1) & last_hop(way, seg, side))
-                    def _():
-                        for g in range(groups):
+                    for g in range(groups):
+                        @pl.when(sends & (t == half - 1) & last_hop(way, seg, side, g))
+                        def _():
                             part(way, slot, seg, side, g).wait_send()
             return 0
 

time: 141 us -> 139 us (0.986)
  the two profiles are of different devices: /device:TPU:2006 before, /device:TPU:86 now
where the time goes in v6:
time: 139 us; the launch traced here: 138 us
  Pallas kernels  138 us (99%)
    pallas_call x1, Pallas kernels, shards(): pl.pallas_call(functools.partial(kernel, n, groups, heads // groups), out...  137 us

profile of v6, /device:TPU:86, one launch (start us, length us, event | category | flops | bytes accessed | tf_op | source)
XLA Modules:
  0.0 138.2 jit_solution(14620205980441618898)
XLA Ops:
  0.6 136.6 %shard_map.103 = (bf16[256,1792]{1,0:T(8,128)(2,1)S(1)}, bf16[2,16,2048]{2,1,0:T(8,128)(2,1)S(1)}, bf16[2,16,2048]{2,1,0:T(8,128)(2,1)S(1)}) custom-call(s32[256]{0:T(256)} %table_hbm.1, s32[3,4]{1,0:T(4,128)} %remap_hbm.1, f32[1,128]{1,0:T(1,128)} %constant.2.clone.freq_hbm, bf16[256,1792]{1,0:T(8,128)(2,1)} %q_hbm.1, bf16[256,2,256]{2,1,0:T(2,128)(2,1)} %sk_hbm.1, ...), custom_call_target="tpu_custom_call" | custom-call | tf_op jit(solution)/shard_map/pallas_call | solution.py:344
  137.2 1.0 shard_map.104
